TPU v7x, 32 devices: a 4x4x1 block of a 4x4x8 slice. The times are simulated.
32 devices in a mesh: rep: 1 (over z), data: 4 (over y), model: 8 (over x, core).
Axes of the slice: x: 4, y: 4, z: 1, core: 2. Of those that a mesh axis runs over, the one named last changes fastest.
The devices are a block of a 4x4x8 slice.
Arguments:
- x: bfloat16 [32, 1024, 2048], P(('rep', 'data'), 'model')
- lengths: int32 [32], P(('rep', 'data'))
- gamma: bfloat16 [2, 2048], P(None, 'data')
- w_in: bfloat16 [2, 2048, 18432], P(None, 'data', 'model')
- w_kv: bfloat16 [2, 2048, 256], P(None, 'data')
- w_out: bfloat16 [2, 10240, 2048], P(None, 'model', 'data')
Outputs:
- output: bfloat16 [32, 1024, 2048], P(('rep', 'data'), 'model')
All inputs are finite; a program needn't handle non-finite values.
Results may differ from a plain program's by a relative error of at most 0.0158209.
Values are sent between devices in bfloat16 or wider.
A program may use at most 768 MiB of HBM per device.

v0:
```python
import functools

import jax
import jax.numpy as jnp
from jax import lax
from jax.experimental import pallas as pl
from jax.experimental.pallas import tpu as pltpu
from jax.sharding import PartitionSpec as P

EPSILON = 1e-6
VMEM_LIMIT = 66_000_000
MESH = pl.DeviceIdType.MESH
BF16, F32 = jnp.bfloat16, jnp.float32

UP, DOWN, FORWARD, FORWARD_B, FIRST, SIDE_UP, SIDE_DOWN, FAR, MATE, SIDE_MATE = range(10)


def rms_norm(x_in, gain):
    x_f32 = x_in.astype(F32)
    inv_rms = lax.rsqrt(jnp.mean(x_f32 * x_f32, axis=-1, keepdims=True) + EPSILON)
    return (x_f32 * inv_rms * gain.astype(F32)).astype(BF16)


class Place:
    def __init__(self, n_data, n_model, partner, neighbour):
        self.n_data, self.n_model = n_data, n_model
        self.y = lax.axis_index("data")
        self.me = lax.axis_index("model")
        self.up = lax.rem(self.y + 1, n_data)
        self.down = lax.rem(self.y + n_data - 1, n_data)
        self.far = lax.rem(self.y + 2, n_data)
        self.slots = (self.y, self.down, self.up, self.far)
        self.mate = self.me + 1 - 2 * lax.rem(self.me, 2)
        self.partner, self.neighbour = partner(self.me), neighbour(self.me)
        n_other = n_model // 2 - 1
        self.ahead = [lax.rem(self.me + 2 * k, n_model) for k in range(1, n_other + 1)]
        self.behind = [lax.rem(self.me + n_model - 2 * k, n_model) for k in range(1, n_other + 1)]

    def meet(self):
        barrier = pltpu.get_barrier_semaphore()
        targets = [{"data": self.up}, {"data": self.down}, {"data": self.far}, {"model": self.mate}]
        targets += [{"model": m} for m in self.ahead]
        for target in targets:
            pl.semaphore_signal(barrier, inc=1, device_id=target, device_id_type=MESH)
        pl.semaphore_wait(barrier, len(targets))


def remote(src, dst, send, recv, target):
    return pltpu.make_async_remote_copy(
        src_ref=src, dst_ref=dst, send_sem=send, recv_sem=recv, device_id=target, device_id_type=MESH
    )


class GatherIn:
    def __init__(self, place, buf, pool, own, send, recv, local, first=None, column=None):
        self.place, self.buf, self.pool, self.own, self.first, self.column = place, buf, pool, own, first, column
        self.send, self.recv, self.local = send, recv, local

    def at(self, block, g, slot):
        return self.buf.at[block, g, slot]

    def _copy(self, src, dst, kind, at, target):
        return remote(src, dst, self.send.at[kind, at], self.recv.at[kind, at], target)

    def up(self, g, half):
        dst = self.at(0, g, self.place.y).at[half]
        return self._copy(self.own(g, half), dst, UP, 2 * g + half, {"data": self.place.up})

    def down(self, g, half):
        dst = self.at(0, g, self.place.y).at[half]
        return self._copy(self.own(g, half), dst, DOWN, 2 * g + half, {"data": self.place.down})

    def neighbour_first(self, g, half):
        dst = self.at(2, g, self.place.y).at[half]
        return self._copy(self.own(g, half), dst, FIRST, 2 * g + half, {"model": self.place.neighbour})

    def forward(self, g, half):
        ref = self.at(0, g, (self.place.down, self.place.up)[half]).at[half]
        target = (self.place.up, self.place.down)[half]
        return self._copy(ref, ref, FORWARD, 2 * g + half, {"data": target})

    def _needed(self, ref, g):
        return ref.at[0] if isinstance(g, int) and g == 0 else ref

    def _side(self, g, kind, target):
        src = self.at(2, g, self.place.y) if self.first is None else self.first.at[g]
        dst = self.at(2, g, self.place.y)
        return self._copy(self._needed(src, g), self._needed(dst, g), kind, g, {"data": target})

    def side_up(self, g):
        return self._side(g, SIDE_UP, self.place.up)

    def side_down(self, g):
        return self._side(g, SIDE_DOWN, self.place.down)

    def far(self, g):
        slot = self.place.far
        src = self.at(0, g, slot) if self.column is None else self.column.at[g, slot]
        dst = self.at(2, g, slot)
        return self._copy(self._needed(src, g), self._needed(dst, g), FAR, g, {"model": self.place.neighbour})

    def mate(self, g):
        return self._copy(self.buf.at[0, g], self.pool.at[0, g], MATE, g, {"model": self.place.mate})

    def side_mate(self, g):
        src, dst = self.buf.at[2, g], self.pool.at[1, g]
        if isinstance(g, int) and g == 0:
            src, dst = src.at[:, 0], dst.at[:, 0]
        return self._copy(src, dst, SIDE_MATE, g, {"model": self.place.mate})

    def load_mate(self, g):
        return pltpu.make_async_copy(self.pool.at[0, g], self.buf.at[1, g], self.local.at[6, g])

    def load_side(self, g):
        src, dst = self.pool.at[1, g], self.buf.at[3, g]
        if isinstance(g, int) and g == 0:
            src, dst = src.at[:, 0], dst.at[:, 0]
        return pltpu.make_async_copy(src, dst, self.local.at[7, g])

    def take_mate(self, g):
        self.mate(g).wait_recv()
        self.load_mate(g).start()

    def take_side(self, g):
        self.side_mate(g).wait_recv()
        self.load_side(g).start()

    def load_own(self, g, half):
        dst = self.at(0, g, self.place.y).at[half]
        return pltpu.make_async_copy(self.own(g, half), dst, self.local.at[half, g])

    def load_column(self, g, which):
        slot = self.place.slots[which]
        return pltpu.make_async_copy(self.column.at[g, slot], self.at(0, g, slot), self.local.at[1 + which, g])

    def load_first(self, g):
        return pltpu.make_async_copy(self.first.at[g], self.at(2, g, self.place.y), self.local.at[5, g])

    def pass_side(self, g):
        if self.first is not None:
            self.load_first(g).wait()
        self.side_up(g).wait_recv()
        self.side_down(g).wait_recv()
        self.far(g).wait_recv()
        self.side_mate(g).start()

    def wait_sends(self, g):
        made = [self.side_up(g), self.side_down(g), self.far(g), self.mate(g), self.side_mate(g)]
        if self.column is None:
            made += [copy(g, half) for copy in (self.up, self.down, self.forward) for half in range(2)]
        if self.first is None:
            made += [self.neighbour_first(g, half) for half in range(2)]
        for copy in made:
            copy.wait_send()


class FetchIn:
    def __init__(self, place, own, send, recv, neighbour=None, first=None, column=None):
        self.place, self.own, self.send, self.recv = place, own, send, recv
        self.neighbour, self.first, self.column = neighbour, first, column

    def _ring(self, g, half, kind, target):
        at = 2 * g + half
        dst = self.column.at[g, self.place.y, half]
        return remote(self.own(g, half), dst, self.send.at[kind, at], self.recv.at[kind, at], {"data": target})

    def up(self, g, half):
        return self._ring(g, half, 0, self.place.up)

    def down(self, g, half):
        return self._ring(g, half, 1, self.place.down)

    def forward(self, g, half):
        at = 2 * g + half
        ref = self.column.at[g, (self.place.down, self.place.up)[half], half]
        target = (self.place.up, self.place.down)[half]
        return remote(ref, ref, self.send.at[2, at], self.recv.at[2, at], {"data": target})

    def ring_stage(self, g):
        for half in range(2):
            self.up(g, half).wait_recv()
            self.down(g, half).wait_recv()
        for half in range(2):
            self.forward(g, half).start()

    def send_slices(self, g):
        for half in range(2):
            self.up(g, half).start()
            self.down(g, half).start()

    def neighbour_first(self, g, half):
        at = 2 * g + half
        dst = self.first.at[g, half]
        return remote(self.own(g, half), dst, self.send.at[3, at], self.recv.at[3, at], {"model": self.neighbour})


class GatherOut:
    def __init__(self, place, buf, own, send, recv, local=None, first=None, column=None, pool=None, whole_column=True):
        self.place, self.buf, self.own, self.first, self.column = place, buf, own, first, column
        self.far_held = column is not None and whole_column
        self.send, self.recv, self.local, self.pool = send, recv, local, pool

    def _copy(self, src, dst, kind, target):
        return remote(src, dst, self.send.at[kind], self.recv.at[kind], target)

    def up(self):
        return self._copy(self.own, self.buf.at[0, self.place.y], UP, {"data": self.place.up})

    def down(self):
        return self._copy(self.own, self.buf.at[0, self.place.y], DOWN, {"data": self.place.down})

    def _half(self, ref, second):
        size = ref.shape[0] // 2
        return ref.at[pl.ds(second * size, size)]

    def _forward(self, kind, slot, second, target):
        src = self.buf if self.column is None else self.column
        dst = self._half(self.buf.at[0, slot], second)
        return self._copy(self._half(src.at[0, slot], second), dst, kind, {"data": target})

    def forward(self):
        return self._forward(FORWARD, self.place.down, 0, self.place.up)

    def forward_b(self):
        return self._forward(FORWARD_B, self.place.up, 1, self.place.down)

    def neighbour_first(self, dst):
        return self._copy(self.own, dst, FIRST, {"model": self.place.neighbour})

    def side_up(self):
        return self._copy(self.first, self.buf.at[2, self.place.y], SIDE_UP, {"data": self.place.up})

    def side_down(self):
        return self._copy(self.first, self.buf.at[2, self.place.y], SIDE_DOWN, {"data": self.place.down})

    def far(self):
        slot = self.place.far
        src = self.column.at[0, slot] if self.far_held else self.buf.at[0, slot]
        return self._copy(src, self.buf.at[2, slot], FAR, {"model": self.place.neighbour})

    def mate(self, which):
        slot = self.place.slots[which]
        if which == 0:
            src = self.own
        else:
            src = self.column.at[0, slot] if which < 3 or self.far_held else self.buf.at[0, slot]
        return self._copy(src, self.pool.at[0, slot], MATE + 2 * which, {"model": self.place.mate})

    def side_mate(self, which):
        slot = self.place.slots[which]
        src = self.first if which == 0 else self.buf.at[2, slot]
        return self._copy(src, self.pool.at[1, slot], SIDE_MATE + 2 * which, {"model": self.place.mate})

    def load_mate(self, which):
        slot = self.place.slots[which]
        return pltpu.make_async_copy(self.pool.at[0, slot], self.buf.at[1, slot], self.local.at[5 + which])

    def load_side(self, which):
        slot = self.place.slots[which]
        return pltpu.make_async_copy(self.pool.at[1, slot], self.buf.at[3, slot], self.local.at[9 + which])

    def take(self, which):
        self.mate(which).wait_recv()
        self.load_mate(which).start()
        self.side_mate(which).wait_recv()
        self.load_side(which).start()

    def load_own(self):
        return pltpu.make_async_copy(self.own, self.buf.at[0, self.place.y], self.local.at[0])

    def load_column(self, which):
        slot = self.place.slots[which]
        return pltpu.make_async_copy(self.column.at[0, slot], self.buf.at[0, slot], self.local.at[which])

    def load_first(self):
        return pltpu.make_async_copy(self.first, self.buf.at[2, self.place.y], self.local.at[4])


def in_halves(layer, w_kv_ref, w_ref, c, ff):
    def own(g, half):
        if isinstance(g, int) and g == 0:
            return w_kv_ref.at[layer] if half else w_ref.at[layer, :, pl.ds(0, c)]
        return w_ref.at[layer, :, pl.ds(pl.multiple_of(g * c + half * ff, c), c)]

    return own


def project(layer, n_data, n_model, partner, neighbour, next_neighbour, x_own, w_kv, w_in, w_out, extra):
    start_layer = layer == 0
    part, c = w_kv.shape[1:]
    d_model = part * n_data
    rows = x_own.size // d_model
    depth, out_part = w_out.shape[1:]
    ff = depth - c
    n_group = 1 + ff // c
    n_units = 8 * n_group
    row_parts = 4
    row_part = rows // row_parts
    n_other = n_model // 2 - 1
    gain_shape = (n_data, 8, part)
    n_tiles = 1 if start_layer else x_own.shape[0] * x_own.shape[1]

    def kernel(*refs):
        x_ref, w_kv_ref, w_ref, wo_ref = refs[:4]
        if start_layer:
            gain_ref = refs[4]
            q_ref, m_ref, kv_ref, pool_ref, gains_ref, out_first_ref, out_column_ref, in_first_ref = refs[5:13]
            first_ref = column_ref = None
            rest = refs[13:]
        else:
            par_ref, gain_ref, first_ref, column_ref = refs[4:8]
            q_ref, m_ref, kv_ref, pool_ref, out_first_ref, out_column_ref = refs[8:14]
            rest = refs[14:]
        wbuf, h_ref, gbuf, stage, kv_stage, send, recv, w_local, next_send, next_recv, late_send, late_recv = rest[:12]
        x_send, x_recv, g_send, g_recv, kv_send, kv_recv, local, out_sem, tile_sem = rest[12:]

        place = Place(n_data, n_model, partner, neighbour)
        place.meet()
        in_own = in_halves(layer, w_kv_ref, w_ref, c, ff)
        w = GatherIn(place, wbuf, pool_ref, in_own, send, recv, w_local, first_ref, column_ref)
        out_next = GatherOut(place, out_column_ref, wo_ref.at[layer], next_send, next_recv)
        if start_layer:
            in_own_next = in_halves(layer + 1, w_kv_ref, w_ref, c, ff)
            in_next = FetchIn(place, in_own_next, late_send, late_recv, next_neighbour(place.me), in_first_ref)

        def c_x(part_no):
            piece = pl.ds(part_no * row_part, row_part)
            return remote(
                x_ref.at[piece], h_ref.at[1, piece], x_send.at[part_no], x_recv.at[part_no], {"model": place.partner}
            )

        def c_gain(which):
            target = {"data": (place.up, place.down, place.far)[which]}
            return remote(gain_ref, gbuf.at[place.y], g_send.at[which], g_recv.at[which], target)

        def c_kv(which):
            ref = kv_ref.at[place.me]
            return remote(ref, ref, kv_send.at[which], kv_recv.at[which], {"model": place.ahead[which]})

        def c_kv_mate(which):
            ref = kv_ref.at[place.me if which == 0 else place.behind[which - 1]]
            at = n_other + which
            return remote(ref, ref, kv_send.at[at], kv_recv.at[at], {"model": place.mate})

        save_kv = pltpu.make_async_copy(kv_stage, kv_ref.at[place.me], local.at[0])
        if start_layer:
            load_x = pltpu.make_async_copy(x_ref, h_ref.at[0], local.at[0])

        def load_tile(side, k):
            chunk, slot = k // n_data, lax.rem(k, n_data)
            src = (x_ref, par_ref)[side].at[chunk, slot]
            height, across = src.shape
            down_to, along = pl.multiple_of(chunk * height, height), pl.multiple_of(slot * across, across)
            return pltpu.make_async_copy(src, h_ref.at[side, pl.ds(down_to, height), pl.ds(along, across)], tile_sem.at[side, k])

        if start_layer:
            load_gain = pltpu.make_async_copy(gain_ref, gbuf.at[place.y], local.at[1])
            for which in range(3):
                c_gain(which).start()
        else:
            load_gain = pltpu.make_async_copy(gain_ref, gbuf, local.at[1])
        def send_slices(g):
            for half in range(2):
                w.up(g, half).start()
                w.down(g, half).start()

        load_gain.start()
        if start_layer:
            load_x.start()
        else:
            for side in range(2):

                @pl.loop(0, n_tiles)
                def _(k):
                    load_tile(side, k).start()

        if start_layer:
            send_slices(0)
            for g in range(n_group):
                for half in range(2):
                    w.neighbour_first(g, half).start()
                    w.load_own(g, half).start()
            for part_no in range(row_parts // 2):
                c_x(part_no).start()
        else:
            for g in range(n_group):
                for half in range(2):
                    w.load_own(g, half).start()
                for which in range(1, 4):
                    w.load_column(g, which).start()
                w.side_up(g).start()
                w.side_down(g).start()
                if g < 2:
                    w.far(g).start()
            for g in range(n_group):
                w.load_first(g).start()

        def ring_stage(g):
            for half in range(2):
                w.up(g, half).wait_recv()
                w.down(g, half).wait_recv()
            for half in range(2):
                w.forward(g, half).start()

        def column_stage(g):
            for half in range(2):
                w.load_own(g, half).wait()
            for which in range(1, 4):
                w.load_column(g, which).wait()
            w.mate(g).start()

        if start_layer:
            for which in range(3):
                c_gain(which).wait_recv()
        load_gain.wait()
        gain = jnp.concatenate([gbuf[k, layer:layer + 1, :] for k in range(n_data)], axis=1)
        if start_layer:
            save_gain = pltpu.make_async_copy(gbuf, gains_ref, local.at[1])
            save_gain.start()
        if start_layer:
            load_x.wait()
        else:

            @pl.loop(0, n_tiles)
            def _(k):
                load_tile(0, k).wait()

        def norm_rows(side, part_no):
            piece = pl.ds(part_no * row_part, row_part)
            h_ref[side, piece] = rms_norm(h_ref[side, piece], gain)

        @pl.loop(0, row_parts)
        def _(part_no):
            norm_rows(0, part_no)

        if start_layer:
            send_slices(1)
            ring_stage(0)
        else:
            column_stage(0)

        halfway, quarter = n_units // 2, n_units // 4

        def out_copy(slot, blk, side, g):
            def to_q():
                return pltpu.make_async_copy(stage.at[slot], q_ref.at[blk, side], out_sem.at[slot])

            def to_m():
                return pltpu.make_async_copy(stage.at[slot], m_ref.at[blk, side, g - 1], out_sem.at[slot])

            return to_q, to_m

        @pl.loop(0, n_units)
        def _(step):
            late = step - halfway
            if start_layer:
                opening, second = step < quarter, (step >= quarter) & (step < halfway)
                ahead = (step == 0) | ((lax.rem(step, 2) == 1) & (step < quarter - 1))
                open_g = jnp.where(ahead, (step + 1) // 2, jnp.where(step == quarter - 1, n_group - 1, step // 2 - 1))
                g = jnp.where(opening, open_g, jnp.where(second, (step - quarter) // 2, late // 4))
                open_blk = jnp.where(ahead, 0, 1)
                blk = jnp.where(opening, open_blk, jnp.where(second, lax.rem(step, 2), 2 + lax.rem(late, 4) // 2))
                side = jnp.where(opening, 0, jnp.where(second, 1, lax.rem(late, 2)))

                @pl.when(opening & (blk == 0))
                def _():
                    for half in range(2):
                        w.forward(g, half).wait_recv()

                    @pl.when(g + 2 < n_group)
                    def _():
                        send_slices(g + 2)

                    @pl.when(g + 1 < n_group)
                    def _():
                        ring_stage(g + 1)

                    @pl.when(g + 2 == n_group)
                    def _():
                        for k in range(n_group):
                            for half in range(2):
                                w.neighbour_first(k, half).wait_recv()
                            w.side_up(k).start()
                            w.side_down(k).start()

                    @pl.when(g == 0)
                    def _():
                        w.far(0).start()

                    @pl.when(g > 0)
                    def _():
                        w.far(g).start()

                    @pl.when(g == 1)
                    def _():
                        for part_no in range(row_parts // 2, row_parts):
                            c_x(part_no).start()

                    for half in range(2):
                        w.load_own(g, half).wait()
                    w.mate(g).start()

                    @pl.when(g > 0)
                    def _():
                        w.take_mate(g - 1)

                @pl.when(step == quarter - 2)
                def _():
                    w.take_mate(n_group - 1)

                @pl.when(opening & (blk == 1))
                def _():
                    w.load_mate(g).wait()

                @pl.when(step == quarter)
                def _():
                    @pl.loop(0, row_parts)
                    def _(part_no):
                        c_x(part_no).wait_recv()
                        norm_rows(1, part_no)

                    out_next.neighbour_first(out_first_ref).start()
                    out_next.up().start()
                    out_next.down().start()
                    for k in range(n_group):
                        for half in range(2):
                            in_next.neighbour_first(k, half).start()
            else:
                g = jnp.where(late < 0, step, late) // 4
                blk = jnp.where(late < 0, 0, 2) + lax.rem(step, 4) // 2
                side = lax.rem(step, 2)

                @pl.when((late < 0) & (lax.rem(step, 4) == 0) & (g + 1 < n_group))
                def _():
                    column_stage(g + 1)

                @pl.when(step == 1)
                def _():
                    @pl.loop(0, n_tiles)
                    def _(k):
                        load_tile(1, k).wait()

                    @pl.loop(0, row_parts)
                    def _(part_no):
                        norm_rows(1, part_no)

                @pl.when((late < 0) & (lax.rem(step, 4) == 1))
                def _():
                    w.take_mate(g)

                @pl.when((late < 0) & (lax.rem(step, 4) == 2))
                def _():
                    w.load_mate(g).wait()

                @pl.when(step == n_units - 6)
                def _():
                    out_next.up().wait_recv()
                    out_next.down().wait_recv()
                    out_next.forward().start()
                    out_next.forward_b().start()

            @pl.when(step == halfway - 2)
            def _():
                w.pass_side(0)

            @pl.when(step == halfway + 1)
            def _():
                w.take_side(0)

            @pl.when((late > 1) & (lax.rem(late, 4) == 1))
            def _():
                w.take_side(g)

            @pl.when((late >= 0) & (lax.rem(late, 4) == 2))
            def _():
                @pl.when(g + 1 < n_group)
                def _():
                    w.pass_side(g + 1)

                @pl.when(g == 0)
                def _():
                    w.load_side(0).wait()

                @pl.when(g > 0)
                def _():
                    w.load_side(g).wait()

            slot = lax.rem(step, 2)
            to_q, to_m = out_copy(slot, blk, side, g)

            @pl.when(step >= 2)
            def _():
                to_q().wait()

            def columns(half):
                return wbuf[blk, g, :, half].reshape(d_model, c)

            @pl.when(g == 0)
            def _():
                q = jnp.dot(h_ref[side], columns(0), preferred_element_type=F32)
                stage[slot] = q.astype(BF16)
                to_q().start()

            @pl.when(g > 0)
            def _():
                h_val = h_ref[side]
                gate = jnp.dot(h_val, columns(0), preferred_element_type=F32).astype(BF16).astype(F32)
                raised = jnp.dot(h_val, columns(1), preferred_element_type=F32).astype(BF16).astype(F32)
                stage[slot] = (gate * jax.nn.sigmoid(gate) * raised).astype(BF16)
                to_m().start()

            @pl.when(step == 0)
            def _():
                kv_stage[...] = jnp.dot(h_ref[0], columns(1), preferred_element_type=F32).astype(BF16)
                save_kv.start()

            @pl.when(step == 1)
            def _():
                save_kv.wait()
                for which in range(n_other):
                    c_kv(which).start()
                c_kv_mate(0).start()
                if not start_layer:
                    for k in range(2, n_group):
                        w.far(k).start()

            @pl.when(step == n_units - 4)
            def _():
                for which in range(n_other):
                    c_kv(which).wait_recv()
                    c_kv_mate(1 + which).start()

            if not start_layer:

                @pl.when(step == 8)
                def _():
                    out_next.up().start()
                    out_next.down().start()
                    out_next.neighbour_first(out_first_ref).start()
        for which in range(n_other + 1):
            c_kv_mate(which).wait()
        for which in range(n_other):
            c_kv(which).wait_send()
        if start_layer:
            save_gain.wait()
            for which in range(3):
                c_gain(which).wait_send()
            for part_no in range(row_parts):
                c_x(part_no).wait_send()
            for g in range(n_group):
                for half in range(2):
                    in_next.neighbour_first(g, half).wait()
            for copy in (out_next.up(), out_next.down()):
                copy.wait()
        else:
            for copy in (out_next.forward(), out_next.forward_b()):
                copy.wait()
            for copy in (out_next.up(), out_next.down()):
                copy.wait_send()
        out_next.neighbour_first(out_first_ref).wait()
        for slot in range(2):
            pltpu.make_async_copy(stage.at[slot], q_ref.at[0, 0], out_sem.at[slot]).wait()

        for g in range(n_group):
            w.wait_sends(g)

    anywhere = pl.BlockSpec(memory_space=pl.ANY)
    out_shape = [
        jax.ShapeDtypeStruct((4, 2, rows, c), BF16),
        jax.ShapeDtypeStruct((4, 2, n_group - 1, rows, c), BF16),
        jax.ShapeDtypeStruct((n_model, rows, c), BF16),
        jax.ShapeDtypeStruct((2, n_group, n_data, 2, part, c), BF16),
    ]
    if start_layer:
        out_shape += [
            jax.ShapeDtypeStruct(gain_shape, F32),
            jax.ShapeDtypeStruct((depth, out_part), BF16),
            jax.ShapeDtypeStruct((1, n_data, depth, out_part), BF16),
            jax.ShapeDtypeStruct((n_group, 2, part, c), BF16),
        ]
    else:
        out_shape += [
            jax.ShapeDtypeStruct((depth, out_part), BF16),
            jax.ShapeDtypeStruct((1, n_data, depth, out_part), BF16),
        ]
    dma = pltpu.SemaphoreType.DMA
    args = (x_own, w_kv, w_in, w_out) + tuple(extra)
    return pl.pallas_call(
        kernel,
        out_shape=out_shape,
        in_specs=[anywhere] * len(args),
        out_specs=[anywhere] * len(out_shape),
        scratch_shapes=[
            pltpu.VMEM((4, n_group, n_data, 2, part, c), BF16),
            pltpu.VMEM((2, rows, d_model), BF16),
            pltpu.VMEM(gain_shape, F32),
            pltpu.VMEM((2, rows, c), BF16),
            pltpu.VMEM((rows, c), BF16),
            dma((SIDE_MATE + 1, 2 * n_group)), dma((SIDE_MATE + 1, 2 * n_group)), dma((8, n_group)),
            dma((FIRST + 1,)), dma((FIRST + 1,)), dma((4, 2 * n_group)), dma((4, 2 * n_group)),
            dma((row_parts,)), dma((row_parts,)), dma((3,)), dma((3,)),
            dma((n_model - 1,)), dma((n_model - 1,)), dma((3,)), dma((2,)), dma((2, n_tiles)),
        ],
        compiler_params=pltpu.CompilerParams(collective_id=2 * layer, has_side_effects=True, vmem_limit_bytes=VMEM_LIMIT),
        cost_estimate=pl.CostEstimate(flops=4 * rows * d_model * 4 * (c + 2 * ff), bytes_accessed=16 * rows * d_model, transcendentals=0),
        name=f"project_{layer}",
    )(*args)


def pick(step, values):
    found = jnp.int32(values[0])
    for at in range(1, len(values)):
        if values[at] != values[at - 1]:
            found = jnp.where(step >= at, jnp.int32(values[at]), found)
    return found


def attend_and_sum(layer, last, n_data, n_model, partner, neighbour, next_partner, lens, q, m, kv, x_own, w_in, w_out, w_kv, first, column):
    n_blocks, _, rows, c = q.shape
    n_mid = m.shape[2]
    ff = n_mid * c
    d_model = w_out.shape[2] * n_data
    tiled = x_own.ndim == 4
    depth, out_part = w_out.shape[1:]
    head_dim = c // 2
    n_batch = lens.shape[0]
    slab_len = rows // n_batch
    chunks = 4
    n_seq = n_batch // chunks
    crow = rows // chunks
    tiles = chunks * n_data
    heads = n_blocks * 2
    qrows = heads * slab_len
    key_rows = 2 * slab_len
    scale = head_dim ** -0.5 * 1.4426950408889634
    part = w_kv.shape[1]
    n_group = 1 + ff // c
    if layer == 0:
        order = [(0, 0), (1, 0), (2, 0), (0, 1), (1, 1), (2, 1), (0, 2), (1, 2), (2, 2)]
        order += [(3, 0), (3, 1), (3, 2), (0, 3), (1, 3), (2, 3), (3, 3)]
        opens = (0, 1, 2, 9)
        side_step, far_step = 2, 11
    else:
        order = [(0, 0), (1, 0), (0, 1), (1, 1), (0, 2), (1, 2), (2, 0), (2, 1), (2, 2), (0, 3), (1, 3), (2, 3)]
        order += [(3, which) for which in range(4)]
        opens = (0, 1, 6, 12)
        side_step, far_step = 1, 8
    flying = 3
    settles = {2: (0,), 3: (1,)}
    for at in range(5, tiles):
        settles[at] = (at - flying,)
    held = sum(len(some) for some in settles.values())
    whole_column = layer > 0

    def kernel(*refs):
        lens_ref, q_ref, m_ref, kv_ref, x_ref, wo_ref, first_ref = refs[:7]
        at = 7
        column_ref = refs[at]
        at += 1
        if not last:
            w_kv_ref, wi_ref = refs[at:at + 2]
            at += 2
        y_ref, pool_ref = refs[at:at + 2]
        at += 2
        if not last:
            par_ref, in_column_ref = refs[at:at + 2]
            at += 2
        (wbuf, obuf, kvb, mbuf, xb, zb, zr, z_stage, s_ref, mx_ref, sum_ref, acc_ref,
         send, recv, w_local, in_send, in_recv, z_send, z_recv, y_send, y_recv, y_save, x_sem, m_sem, local) = refs[at:]

        place = Place(n_data, n_model, partner, neighbour)
        place.meet()
        w = GatherOut(place, wbuf, wo_ref.at[layer], send, recv, w_local, first_ref, column_ref, pool_ref, whole_column)

        def tile_of(k):
            which = pick(k, [one for _, one in order])
            slot = jnp.where(which == 0, place.y, jnp.where(which == 1, place.down, jnp.where(which == 2, place.up, place.far)))
            return pick(k, [one for one, _ in order]), which, slot

        def whole(ref, chunk, slot):
            return ref.at[pl.ds(pl.multiple_of(chunk * crow, crow), crow), pl.ds(pl.multiple_of(slot * out_part, out_part), out_part)]

        def rows_of(chunk):
            return pl.ds(pl.multiple_of(chunk * crow, crow), crow)

        def load_q(chunk):
            return pltpu.make_async_copy(q_ref.at[:, :, rows_of(chunk)], obuf.at[:, :, rows_of(chunk)], local.at[0, chunk])

        def load_kv(chunk):
            return pltpu.make_async_copy(kv_ref.at[:, rows_of(chunk)], kvb.at[:, rows_of(chunk)], local.at[1, chunk])

        def load_m(k):
            chunk, _, _ = tile_of(k)
            slot = lax.rem(k, 2)
            return pltpu.make_async_copy(
                m_ref.at[:, :, :, pl.ds(pl.multiple_of(chunk * crow, crow), crow)], mbuf.at[slot], m_sem.at[slot]
            )

        def load_x(k):
            chunk, _, slot = tile_of(k)
            src = x_ref.at[chunk, slot] if tiled else whole(x_ref, chunk, slot)
            return pltpu.make_async_copy(src, xb.at[chunk, slot], x_sem.at[k])

        def c_z(k):
            chunk, _, slot = tile_of(k)
            return remote(z_stage.at[lax.rem(k, 4)], zr.at[chunk, slot], z_send.at[k], z_recv.at[k], {"model": place.partner})

        def c_y(k):
            chunk, _, slot = tile_of(k)
            target = {"model": next_partner(place.me)}
            return remote(xb.at[chunk, slot], par_ref.at[chunk, slot], y_send.at[k], y_recv.at[k], target)

        def save_y(k):
            chunk, _, slot = tile_of(k)
            dst = whole(y_ref, chunk, slot) if last else y_ref.at[chunk, slot]
            return pltpu.make_async_copy(xb.at[chunk, slot], dst, y_save.at[k])

        for chunk in range(chunks):
            load_q(chunk).start()
            load_kv(chunk).start()
        load_m(0).start()
        w.load_own().start()
        w.load_first().start()
        w.mate(0).start()
        w.side_mate(0).start()
        for which in range(1, 4 if whole_column else 3):
            w.load_column(which).start()
            w.mate(which).start()
        w.side_up().start()
        w.side_down().start()
        if whole_column:
            w.far().start()
        else:
            w.forward().start()
            w.forward_b().start()
        if not last:
            in_own = in_halves(layer + 1, w_kv_ref, wi_ref, c, ff)
            in_next = FetchIn(place, in_own, in_send, in_recv, column=in_column_ref)

        @pl.loop(0, tiles)
        def _(k):
            load_x(k).start()

        def attend_one(batch, side):
            slab = jnp.where(side == 0, place.me, place.partner)
            length = lens_ref[batch]
            n_key = slab // 2 + 1
            at_row = pl.ds(pl.multiple_of(batch * slab_len, slab_len), slab_len)
            parts = []
            for blk in range(n_blocks):
                for one in range(2):
                    parts.append(obuf[blk, side, at_row, one * head_dim:(one + 1) * head_dim])
            q_val = jnp.concatenate(parts, axis=0)
            row_pos = slab * slab_len + lax.rem(lax.broadcasted_iota(jnp.int32, (qrows, key_rows), 0), slab_len)
            key_pos = lax.broadcasted_iota(jnp.int32, (qrows, key_rows), 1)
            room = jnp.minimum(row_pos + 1, length) - key_pos
            mx_ref[...] = jnp.full_like(mx_ref, -1e30)

            def score(kb, carry):
                k = kvb[pl.ds(2 * kb, 2), at_row, :head_dim].reshape(key_rows, head_dim)
                s = lax.dot_general(q_val, k, (((1,), (1,)), ((), ())), preferred_element_type=F32) * scale
                s = jnp.where(room > kb * key_rows, s, -1e30)
                s_ref[kb] = s
                mx_ref[...] = jnp.maximum(mx_ref[...], jnp.maximum(s[:, :slab_len], s[:, slab_len:]))
                return carry

            lax.fori_loop(0, n_key, score, 0)
            top = jnp.max(mx_ref[...], axis=-1, keepdims=True)
            mx_ref[...] = jnp.broadcast_to(top, mx_ref.shape)
            sum_ref[...] = jnp.zeros_like(sum_ref)
            acc_ref[...] = jnp.zeros_like(acc_ref)

            def weigh(kb, carry):
                v = kvb[pl.ds(2 * kb, 2), at_row, head_dim:].reshape(key_rows, head_dim)
                top_b = mx_ref[...]
                e_lo = jnp.exp2(s_ref[kb, :, :slab_len] - top_b)
                e_hi = jnp.exp2(s_ref[kb, :, slab_len:] - top_b)
                sum_ref[...] += e_lo + e_hi
                e = jnp.concatenate([e_lo, e_hi], axis=1).astype(BF16)
                acc_ref[...] += jnp.dot(e, v, preferred_element_type=F32)
                return carry

            lax.fori_loop(0, n_key, weigh, 0)
            out = (acc_ref[...] / jnp.sum(sum_ref[...], axis=-1, keepdims=True)).astype(BF16)
            for blk in range(n_blocks):
                for one in range(2):
                    first_row = (blk * 2 + one) * slab_len
                    obuf[blk, side, at_row, one * head_dim:(one + 1) * head_dim] = out[first_row:first_row + slab_len]

        def settle(k):
            chunk, _, slot = tile_of(k)
            load_x(k).wait()
            c_z(k).wait_recv()
            z = zb[chunk, slot].astype(F32) + zr[chunk, slot].astype(F32)
            xb[chunk, slot] = (xb[chunk, slot].astype(F32) + z).astype(BF16)
            save_y(k).start()
            if not last:
                c_y(k).start()

        @pl.loop(0, tiles)
        def _(step):
            chunk, which, slot = tile_of(step)

            @pl.when(step + 1 < tiles)
            def _():
                load_m(step + 1).start()

            opening = functools.reduce(lambda one, other: one | other, [step == at for at in opens])

            @pl.when(opening)
            def _():
                load_q(chunk).wait()
                load_kv(chunk).wait()

                @pl.loop(0, 2 * n_seq)
                def _(unit):
                    attend_one(chunk * n_seq + unit // 2, lax.rem(unit, 2))

            @pl.when(step == 0)
            def _():
                w.load_own().wait()
                w.load_first().wait()
                w.take(0)
                w.load_mate(0).wait()
                w.load_side(0).wait()

            @pl.when(step == side_step)
            def _():
                w.side_up().wait_recv()
                w.side_mate(1).start()
                w.side_down().wait_recv()
                w.side_mate(2).start()

            @pl.when(step == side_step + 1)
            def _():
                for one in (1, 2):
                    w.take(one)
                for one in (1, 2):
                    w.load_column(one).wait()
                    w.load_mate(one).wait()
                    w.load_side(one).wait()

            if not whole_column:

                @pl.when(step == side_step + 2)
                def _():
                    w.forward().wait_recv()
                    w.forward_b().wait_recv()
                    w.far().start()
                    w.mate(3).start()

            @pl.when(step == far_step)
            def _():
                w.far().wait_recv()
                w.side_mate(3).start()

            @pl.when(step == far_step + 1)
            def _():
                w.take(3)
                if whole_column:
                    w.load_column(3).wait()
                w.load_mate(3).wait()
                w.load_side(3).wait()

            if not last:
                for g, at in enumerate((3, 3, 4, 5, 6)[:n_group]):

                    @pl.when(step == at)
                    def _(g=g):
                        in_next.send_slices(g)

                for g, at in enumerate((9, 10, 12, 15)[:n_group]):

                    @pl.when(step == at)
                    def _(g=g):
                        in_next.ring_stage(g)

            @pl.when(step >= flying)
            def _():
                c_z(step - flying).wait_send()

            load_m(step).wait()
            here = lax.rem(step, 2)
            rows_c = pl.ds(pl.multiple_of(chunk * crow, crow), crow)
            total = None
            for blk in range(n_blocks):
                mid = jnp.concatenate([mbuf[here, blk, :, k].reshape(2 * crow, c) for k in range(n_mid)], axis=1)
                attn = obuf[blk, :, rows_c, :].reshape(2 * crow, c)
                one = jnp.dot(mid, wbuf[blk, slot, c:, :], preferred_element_type=F32)
                one = one + jnp.dot(attn, wbuf[blk, slot, :c, :], preferred_element_type=F32)
                total = one if total is None else total + one
            z = total.astype(BF16)
            zb[chunk, slot] = z[:crow]
            z_stage[lax.rem(step, 4)] = z[crow:]
            c_z(step).start()

            for at, some in settles.items():

                @pl.when(step == at)
                def _(some=some):
                    for k in some:
                        settle(k)

        stages = list(range(4, n_group)) if not last else []
        for k in range(held, tiles):
            if stages and k - held >= 2:
                in_next.ring_stage(stages.pop(0))
            settle(k)
        for g in stages:
            in_next.ring_stage(g)

        @pl.loop(0, tiles)
        def _(k):
            save_y(k).wait()
            if not last:
                c_y(k).wait()

        @pl.loop(tiles - flying, tiles)
        def _(k):
            c_z(k).wait_send()

        made = [w.side_up(), w.side_down(), w.far()]
        made += [w.mate(which) for which in range(4)] + [w.side_mate(which) for which in range(4)]
        if not whole_column:
            made += [w.forward(), w.forward_b()]
        for copy in made:
            copy.wait_send()
        if not last:

            @pl.loop(0, n_group)
            def _(g):
                for half in range(2):
                    in_next.forward(g, half).wait()
                    in_next.up(g, half).wait_send()
                    in_next.down(g, half).wait_send()

    anywhere = pl.BlockSpec(memory_space=pl.ANY)
    args = [lens, q, m, kv, x_own, w_out, first, column]
    if not last:
        args += [w_kv, w_in]
    tile = (chunks, n_data, crow, out_part)
    out_shape = [
        jax.ShapeDtypeStruct((rows, d_model) if last else tile, BF16),
        jax.ShapeDtypeStruct((2, n_data, depth, out_part), BF16),
    ]
    if not last:
        out_shape += [
            jax.ShapeDtypeStruct(tile, BF16),
            jax.ShapeDtypeStruct((n_group, n_data, 2, part, c), BF16),
        ]
    dma = pltpu.SemaphoreType.DMA
    return pl.pallas_call(
        kernel,
        out_shape=out_shape,
        in_specs=[pl.BlockSpec(memory_space=pltpu.SMEM)] + [anywhere] * (len(args) - 1),
        out_specs=[anywhere] * len(out_shape),
        scratch_shapes=[
            pltpu.VMEM((n_blocks, n_data, depth, out_part), BF16),
            pltpu.VMEM(q.shape, BF16),
            pltpu.VMEM(kv.shape, BF16),
            pltpu.VMEM((2, n_blocks, 2, n_mid, crow, c), BF16),
            pltpu.VMEM(tile, BF16),
            pltpu.VMEM(tile, BF16),
            pltpu.VMEM(tile, BF16),
            pltpu.VMEM((4, crow, out_part), BF16),
            pltpu.VMEM((n_model // 2, qrows, key_rows), F32),
            pltpu.VMEM((qrows, slab_len), F32),
            pltpu.VMEM((qrows, slab_len), F32),
            pltpu.VMEM((qrows, head_dim), F32),
            dma((SIDE_MATE + 7,)), dma((SIDE_MATE + 7,)), dma((13,)), dma((3, 2 * n_group)), dma((3, 2 * n_group)),
            dma((tiles,)), dma((tiles,)), dma((tiles,)), dma((tiles,)), dma((tiles,)), dma((tiles,)), dma((2,)), dma((2, chunks)),
        ],
        compiler_params=pltpu.CompilerParams(collective_id=2 * layer + 1, has_side_effects=True, vmem_limit_bytes=VMEM_LIMIT),
        cost_estimate=pl.CostEstimate(flops=4 * rows * n_blocks * depth * d_model, bytes_accessed=16 * rows * d_model, transcendentals=0),
        name=f"attend_and_sum_{layer}",
    )(*args)


def solution(mesh):
    batch_axes = ("rep", "data")
    n_data, n_model = mesh.shape["data"], mesh.shape["model"]
    n_chip = n_model // 2

    def near(x):
        return x + 1 - 2 * (x % 2)

    def across(x):
        return n_chip - 1 - x

    def on_chip(other):
        return lambda m: 2 * other(m // 2) + m % 2

    def local_step(x_loc, lens_loc, gamma_loc, w_in_loc, w_kv_loc, w_out_loc):
        n_batch, slab_len, d_model = x_loc.shape
        n_layers, part = gamma_loc.shape
        partners = [on_chip(near if layer % 2 == 0 else across) for layer in range(n_layers)]
        neighbours = [on_chip(across if layer % 2 == 0 else near) for layer in range(n_layers)]

        gain_rows = jnp.zeros((8, part), F32).at[:n_layers].set(gamma_loc.astype(F32))
        own = x_loc.reshape(n_batch * slab_len, d_model)
        for layer in range(n_layers):
            last = layer + 1 == n_layers
            following = min(layer + 1, n_layers - 1)
            if layer == 0:
                extra = (gain_rows,)
                q, m, kv, _, gains, out_first, out_column, in_first = project(
                    layer, n_data, n_model, partners[layer], neighbours[layer], neighbours[following],
                    own, w_kv_loc, w_in_loc, w_out_loc, extra,
                )
            else:
                extra = (other, gains, in_first, in_column)
                q, m, kv, _, out_first, out_column = project(
                    layer, n_data, n_model, partners[layer], neighbours[layer], neighbours[following],
                    own, w_kv_loc, w_in_loc, w_out_loc, extra,
                )
            outs = attend_and_sum(
                layer, last, n_data, n_model, partners[layer], neighbours[layer], partners[following],
                lens_loc, q, m, kv, own, w_in_loc, w_out_loc, w_kv_loc, out_first, out_column,
            )
            own = outs[0]
            if not last:
                other, in_column = outs[2:]
        return own.reshape(n_batch, slab_len, d_model)

    in_specs = (
        P(batch_axes, "model", None),
        P(batch_axes),
        P(None, "data"),
        P(None, "data", "model"),
        P(None, "data", None),
        P(None, "model", "data"),
    )
    return jax.shard_map(local_step, mesh=mesh, in_specs=in_specs, out_specs=P(batch_axes, "model", None), check_vma=False)
```

profile of v0, /device:TPU:97, one launch (start us, length us, event | category | flops | bytes accessed | tf_op | source)
XLA Modules:
  0.0 595.7 jit_solution(9559964667950301356)
XLA Ops:
  0.0 1.3 pad_convert_fusion.refs_4_
  1.3 182.4 %project_0.1 = (bf16[4,2,1024,256]{3,2,1,0:T(8,128)(2,1)}, bf16[4,2,4,1024,256]{4,3,2,1,0:T(8,128)(2,1)}, bf16[8,1024,256]{2,1,0:T(8,128)(2,1)}, bf16[2,5,4,2,51...) custom-call(bf16[1024,2048]{1,0:T(8,128)(2,1)} %bitcast.3, ...), custom_call_target="tpu_custom_call" | custom-call | flops 77309411328 | bytes 33554432 | tf_op jit(solution)/shard_map/project_0/pallas_call | solution.py:688
  183.7 174.6 %attend_and_sum_0.1 = (bf16[4,4,256,512]{3,2,1,0:T(8,128)(2,1)}, bf16[2,4,1280,512]{3,2,1,0:T(8,128)(2,1)}, bf16[4,4,256,512]{3,2,1,0:T(8,128)(2,1)}, bf16[5,4,2,512,256]{4,3,2,1,0:T(8,128)(2,1)}) custom-call(s32[8]{0:T(128)} %refs_0_.3, bf16[4,2,1024,256]{3,2,1,0:T(8,128)(2,1)} %get-tuple-element.33.refs_1_, ...), custom_call_target="tpu_custom_call" | custom-call | flops 42949672960 | bytes 33554432 | tf_op jit(solution)/shard_map/attend_and_sum_0/pallas_call | solution.py:1052
  358.4 106.5 %project_1.1 = (bf16[4,2,1024,256]{3,2,1,0:T(8,128)(2,1)}, bf16[4,2,4,1024,256]{4,3,2,1,0:T(8,128)(2,1)}, bf16[8,1024,256]{2,1,0:T(8,128)(2,1)}, bf16[2,5,4,2,51...) custom-call(bf16[4,4,256,512]{3,2,1,0:T(8,128)(2,1)} %get-tuple-element.38.refs_0_.refs_4_, ...), custom_call_target="tpu_custom_call" | custom-call | flops 77309411328 | bytes 33554432 | tf_op jit(solution)/shard_map/project_1/pallas_call | solution.py:688
  464.9 126.0 %attend_and_sum_1.1 = (bf16[1024,2048]{1,0:T(8,128)(2,1)}, bf16[2,4,1280,512]{3,2,1,0:T(8,128)(2,1)}) custom-call(s32[8]{0:T(128)} %refs_0_.3, bf16[4,2,1024,256]{3,2,1,0:T(8,128)(2,1)} %get-tuple-element.43.refs_1_, bf16[4,2,4,1024,256]{4,3,2,1,0:T(8,128)(2,1)} %get-tuple-element.44.refs_2_, bf16[8,1024,256]{2,1,0:T(8,128)(2,1)} %get-tuple-element.45.refs_3_, ...), custom_call_target="tpu_custom_call" | custom-call | flops 42949672960 | bytes 33554432 | tf_op jit(solution)/shard_map/attend_and_sum_1/pallas_call | solution.py:1052
  590.9 4.8 copy.8
where the time goes:
time: 596 us
  Pallas kernels  590 us (99%)
    pallas_call x2, Pallas kernels, attend_and_sum(): pl.pallas_call(kernel, out_shape=out_shape, in_specs=[pl.BlockSpec(memory...  301 us
    pallas_call x2, Pallas kernels, project(): pl.pallas_call(kernel, out_shape=out_shape, in_specs=[anywhere] * len(arg...  289 us

commit v1 on v0

--- a/solution.py
+++ b/solution.py
@@ -826,13 +826,13 @@
         for which in range(1, 4 if whole_column else 3):
             w.load_column(which).start()
             w.mate(which).start()
-        w.side_up().start()
-        w.side_down().start()
         if whole_column:
             w.far().start()
         else:
             w.forward().start()
             w.forward_b().start()
+        w.side_up().start()
+        w.side_down().start()
         if not last:
             in_own = in_halves(layer + 1, w_kv_ref, wi_ref, c, ff)
             in_next = FetchIn(place, in_own, in_send, in_recv, column=in_column_ref)
@@ -942,7 +942,7 @@
 
             if not whole_column:
 
-                @pl.when(step == side_step + 2)
+                @pl.when(step == side_step - 1)
                 def _():
                     w.forward().wait_recv()
                     w.forward_b().wait_recv()

time: 596 us -> 577 us (0.968)
  Pallas kernels: 590 us -> 570 us
    pallas_call x2, Pallas kernels: 301 us -> 281 us  [attend_and_sum(): pl.pallas_call(kernel, out_shape=out_shape, in_specs=[pl.BlockSpec(memory...]
where the time goes in v1:
time: 577 us; the launch traced here: 576 us
  Pallas kernels  570 us (99%)
    pallas_call x2, Pallas kernels, project(): pl.pallas_call(kernel, out_shape=out_shape, in_specs=[anywhere] * len(arg...  289 us
    pallas_call x2, Pallas kernels, attend_and_sum(): pl.pallas_call(kernel, out_shape=out_shape, in_specs=[pl.BlockSpec(memory...  281 us

profile of v1, /device:TPU:97, one launch (start us, length us, event | category | flops | bytes accessed | tf_op | source)
XLA Modules:
  0.0 576.3 jit_solution(2723627918941352659)
XLA Ops:
  0.0 1.3 pad_convert_fusion.refs_4_
  1.3 182.4 %project_0.1 = (bf16[4,2,1024,256]{3,2,1,0:T(8,128)(2,1)}, bf16[4,2,4,1024,256]{4,3,2,1,0:T(8,128)(2,1)}, bf16[8,1024,256]{2,1,0:T(8,128)(2,1)}, bf16[2,5,4,2,51...) custom-call(bf16[1024,2048]{1,0:T(8,128)(2,1)} %bitcast.3, ...), custom_call_target="tpu_custom_call" | custom-call | flops 77309411328 | bytes 33554432 | tf_op jit(solution)/shard_map/project_0/pallas_call | solution.py:688
  183.7 155.1 %attend_and_sum_0.1 = (bf16[4,4,256,512]{3,2,1,0:T(8,128)(2,1)}, bf16[2,4,1280,512]{3,2,1,0:T(8,128)(2,1)}, bf16[4,4,256,512]{3,2,1,0:T(8,128)(2,1)}, bf16[5,4,2,512,256]{4,3,2,1,0:T(8,128)(2,1)}) custom-call(s32[8]{0:T(128)} %refs_0_.3, bf16[4,2,1024,256]{3,2,1,0:T(8,128)(2,1)} %get-tuple-element.33.refs_1_, ...), custom_call_target="tpu_custom_call" | custom-call | flops 42949672960 | bytes 33554432 | tf_op jit(solution)/shard_map/attend_and_sum_0/pallas_call | solution.py:1052
  338.9 106.5 %project_1.1 = (bf16[4,2,1024,256]{3,2,1,0:T(8,128)(2,1)}, bf16[4,2,4,1024,256]{4,3,2,1,0:T(8,128)(2,1)}, bf16[8,1024,256]{2,1,0:T(8,128)(2,1)}, bf16[2,5,4,2,51...) custom-call(bf16[4,4,256,512]{3,2,1,0:T(8,128)(2,1)} %get-tuple-element.38.refs_0_.refs_4_, ...), custom_call_target="tpu_custom_call" | custom-call | flops 77309411328 | bytes 33554432 | tf_op jit(solution)/shard_map/project_1/pallas_call | solution.py:688
  445.4 126.0 %attend_and_sum_1.1 = (bf16[1024,2048]{1,0:T(8,128)(2,1)}, bf16[2,4,1280,512]{3,2,1,0:T(8,128)(2,1)}) custom-call(s32[8]{0:T(128)} %refs_0_.3, bf16[4,2,1024,256]{3,2,1,0:T(8,128)(2,1)} %get-tuple-element.43.refs_1_, bf16[4,2,4,1024,256]{4,3,2,1,0:T(8,128)(2,1)} %get-tuple-element.44.refs_2_, bf16[8,1024,256]{2,1,0:T(8,128)(2,1)} %get-tuple-element.45.refs_3_, ...), custom_call_target="tpu_custom_call" | custom-call | flops 42949672960 | bytes 33554432 | tf_op jit(solution)/shard_map/attend_and_sum_1/pallas_call | solution.py:1052
  571.5 4.8 copy.8
